TPU v7x, 32 devices: a whole 2x2x4 slice. The times are simulated.
32 devices in a mesh: cuts: 4 (over x, core), exp: 2 (over y), fsdp: 4 (over z).
Axes of the slice: x: 2, y: 2, z: 4, core: 2. Of those that a mesh axis runs over, the one named last changes fastest.
Arguments:
- tokens: bfloat16 [4096, 4096], P(('cuts', 'exp', 'fsdp')), may hold values from -6 to 6
- out_grad: bfloat16 [4096, 4096], P(('cuts', 'exp', 'fsdp')), may hold values from -6 to 6
- expert_ids: int32 [4096, 2], P(('cuts', 'exp', 'fsdp')), may hold values from 0 to 7, as said below
- gate_probs: bfloat16 [4096, 2], P(('cuts', 'exp', 'fsdp')), may hold values from 0.049804688 to 0.94921875
- params: float32 [3, 8, 4096, 256], P(None, 'exp', ('cuts', 'fsdp')), may hold values from -0.1875 to 0.1875
- moment_first: float32 [3, 8, 4096, 256], P(None, 'exp', ('cuts', 'fsdp')), may hold values from -60 to 60
- moment_second: float32 [3, 8, 4096, 256], P(None, 'exp', ('cuts', 'fsdp')), may hold values from 64 to 1024
Outputs:
- token_grad: bfloat16 [4096, 4096], P(('cuts', 'exp', 'fsdp'))
- gate_grad: bfloat16 [4096, 2], P(('cuts', 'exp', 'fsdp'))
- new_params: float32 [3, 8, 4096, 256], P(None, 'exp', ('cuts', 'fsdp'))
- new_first: float32 [3, 8, 4096, 256], P(None, 'exp', ('cuts', 'fsdp'))
- new_second: float32 [3, 8, 4096, 256], P(None, 'exp', ('cuts', 'fsdp'))
Inputs may be any that keep to these rules, and one draw needn't show every extreme that they name: `expert_ids`: the two ids of a token differ. Among the tokens of one device no expert is named more than 40 times. Each device names some expert exactly 40 times, and the devices that share their cuts and fsdp indices have one such expert in common.
All inputs are finite; a program needn't handle non-finite values.
Results may differ from a plain program's by a relative error of at most 0.0079.
Values may be sent and summed in bfloat16 or wider, within the bound.
A program may use at most 192 MiB of HBM per device.

v0:
```python
import jax
import jax.numpy as jnp
from jax import lax
from jax.sharding import PartitionSpec as P

EXPERTS = 8
decay_first = 0.9
decay_second = 0.95
correct_first = 1.0 - 0.9**10
correct_second = 1.0 - 0.95**10
epsilon = 1e-08
learn_rate = 0.0003
weight_decay = 0.1


def adam_update(params, gradient, moment_first, moment_second):
    new_first = decay_first * moment_first + (1.0 - decay_first) * gradient
    new_second = decay_second * moment_second + (1.0 - decay_second) * gradient * gradient
    stepped = new_first / correct_first / (jnp.sqrt(new_second / correct_second) + epsilon)
    new_params = params - learn_rate * (stepped + weight_decay * params)
    return (new_params, new_first, new_second)


def per_device(tokens, out_grad, expert_ids, gate_probs, params, moment_first, moment_second):
    token_count = tokens.shape[0]
    width = tokens.shape[1]
    local_count = params.shape[1]
    exp_count = lax.axis_size("exp")
    capacity = 10 * token_count // 32
    weights = lax.all_gather(params.astype(jnp.bfloat16), ("cuts", "fsdp"), axis=2, tiled=True)
    flat_ids = expert_ids.reshape(-1)
    onehot = (flat_ids[:, None] == jnp.arange(EXPERTS, dtype=jnp.int32)[None, :]).astype(jnp.int32)
    before = jnp.cumsum(onehot, axis=0) - onehot
    position = jnp.sum(before * onehot, axis=1)
    holder = flat_ids // local_count
    local_index = flat_ids % local_count
    target = (local_index * exp_count + holder) * capacity + position
    placement = (
        target[:, None] == jnp.arange(EXPERTS * capacity, dtype=jnp.int32)[None, :]
    ).astype(jnp.bfloat16)
    token_place = jnp.sum(placement.reshape(token_count, 2, EXPERTS * capacity), axis=1)
    send_inputs = jnp.einsum(
        "tc,td->cd", token_place, tokens, preferred_element_type=jnp.float32
    ).astype(jnp.bfloat16)
    send_upstream = jnp.einsum(
        "tc,td->cd", token_place, out_grad, preferred_element_type=jnp.float32
    ).astype(jnp.bfloat16)
    send_gates = jnp.einsum(
        "pc,p->c", placement, gate_probs.reshape(-1), preferred_element_type=jnp.float32
    ).astype(jnp.bfloat16)
    layout = (local_count, exp_count, capacity)
    arrived_inputs, arrived_upstream, arrived_gates = (
        lax.all_to_all(
            send_inputs.reshape(layout + (width,)), "exp", split_axis=1, concat_axis=1, tiled=True
        ),
        lax.all_to_all(
            send_upstream.reshape(layout + (width,)), "exp", split_axis=1, concat_axis=1, tiled=True
        ),
        lax.all_to_all(
            send_gates.reshape(layout + (1,)), "exp", split_axis=1, concat_axis=1, tiled=True
        ),
    )
    slot_count = exp_count * capacity
    arrived_inputs = arrived_inputs.reshape(local_count, slot_count, width)
    arrived_upstream = arrived_upstream.reshape(local_count, slot_count, width)
    gate_values = arrived_gates.reshape(local_count, slot_count, 1).astype(jnp.float32)
    w_gate = weights[0]
    w_up = weights[1]
    w_down = weights[2]
    pre_gate = jnp.einsum(
        "esd,edf->esf", arrived_inputs, w_gate, preferred_element_type=jnp.float32
    )
    pre_up = jnp.einsum("esd,edf->esf", arrived_inputs, w_up, preferred_element_type=jnp.float32)
    sigmoid_gate = jax.nn.sigmoid(pre_gate)
    activated = pre_gate * sigmoid_gate
    hidden = activated * pre_up
    projected = jnp.einsum(
        "esd,edf->esf", arrived_upstream, w_down, preferred_element_type=jnp.float32
    )
    slot_gate = jnp.sum(hidden * projected, axis=2, keepdims=True).astype(jnp.bfloat16)
    delta_hidden = gate_values * projected
    delta_gate = (
        delta_hidden * pre_up * sigmoid_gate * (1.0 + pre_gate * (1.0 - sigmoid_gate))
    ).astype(jnp.bfloat16)
    delta_up = (delta_hidden * activated).astype(jnp.bfloat16)
    scaled = (gate_values * arrived_upstream.astype(jnp.float32)).astype(jnp.bfloat16)
    slot_grads = (
        jnp.einsum("esf,edf->esd", delta_gate, w_gate, preferred_element_type=jnp.float32)
        + jnp.einsum("esf,edf->esd", delta_up, w_up, preferred_element_type=jnp.float32)
    ).astype(jnp.bfloat16)
    returned_grads, returned_gate = (
        lax.all_to_all(
            slot_grads.reshape(layout + (width,)), "exp", split_axis=1, concat_axis=1, tiled=True
        ),
        lax.all_to_all(
            slot_gate.reshape(layout + (1,)), "exp", split_axis=1, concat_axis=1, tiled=True
        ),
    )
    grad_gate = jnp.einsum(
        "esd,esf->edf", arrived_inputs, delta_gate, preferred_element_type=jnp.float32
    )
    grad_up = jnp.einsum(
        "esd,esf->edf", arrived_inputs, delta_up, preferred_element_type=jnp.float32
    )
    grad_down = jnp.einsum(
        "esd,esf->edf", scaled, hidden.astype(jnp.bfloat16), preferred_element_type=jnp.float32
    )
    returned_grads = returned_grads.reshape(EXPERTS * capacity, width)
    returned_gate = returned_gate.reshape(EXPERTS * capacity, 1)
    token_grad = jnp.einsum(
        "tc,cd->td", token_place, returned_grads, preferred_element_type=jnp.float32
    ).astype(jnp.bfloat16)
    gate_grad = jnp.einsum(
        "pc,cx->px", placement, returned_gate, preferred_element_type=jnp.float32
    )
    gate_grad = gate_grad.reshape(token_count, 2).astype(jnp.bfloat16)
    reduced = (
        lax.psum_scatter(grad_gate, ("cuts", "fsdp"), scatter_dimension=1, tiled=True),
        lax.psum_scatter(grad_up, ("cuts", "fsdp"), scatter_dimension=1, tiled=True),
        lax.psum_scatter(grad_down, ("cuts", "fsdp"), scatter_dimension=1, tiled=True),
    )
    gradient = jnp.stack([reduced[0], reduced[1], reduced[2]])
    new_params, new_first, new_second = adam_update(params, gradient, moment_first, moment_second)
    return (token_grad, gate_grad, new_params, new_first, new_second)


def solution(mesh):
    return jax.shard_map(
        per_device,
        mesh=mesh,
        in_specs=(
            P(("cuts", "exp", "fsdp"), None),
            P(("cuts", "exp", "fsdp"), None),
            P(("cuts", "exp", "fsdp"), None),
            P(("cuts", "exp", "fsdp"), None),
            P(None, "exp", ("cuts", "fsdp"), None),
            P(None, "exp", ("cuts", "fsdp"), None),
            P(None, "exp", ("cuts", "fsdp"), None),
        ),
        out_specs=(
            P(("cuts", "exp", "fsdp"), None),
            P(("cuts", "exp", "fsdp"), None),
            P(None, "exp", ("cuts", "fsdp"), None),
            P(None, "exp", ("cuts", "fsdp"), None),
            P(None, "exp", ("cuts", "fsdp"), None),
        ),
        check_vma=False,
    )
```

profile of v0, /device:TPU:0, one launch (start us, length us, event | category | flops | bytes accessed | tf_op | source)
XLA Modules:
  0.0 720.5 jit_solution(18314282270735941708)
XLA Ops:
  7.2 3.3 convert_element_type.82
  12.6 0.6 copy.73
  13.2 4.3 all-to-all-start
  18.0 0.8 convolution_convert_fusion
  18.8 1.8 copy.77
  20.6 0.6 all-to-all-done
  21.2 3.9 all-to-all-start.2
  25.1 2.1 convolution_convert_fusion.1
  27.2 1.8 copy.75
  29.0 26.4 %all-to-all-done.2 = bf16[4,2,40,4096]{3,2,0,1:T(8,128)(2,1)S(1)} async-done(((bf16[4,2,40,4096]{3,2,0,1:T(8,128)(2,1)}), bf16[4,2,40,4096]{3,2,0,1:T(8,128)(2,1)S(1)}, u32[]{:S(2)}, u32[]{:S(2)}) %all-to-all-start.2) | async-done | bytes 2621472 | tf_op jit(solution)/shard_map/all_to_all | solution.py:53
  55.4 5.1 all-to-all-start.1
  60.6 1.9 copy.78
  62.6 27.5 %all-to-all-done.1 = bf16[4,2,40,4096]{3,2,0,1:T(8,128)(2,1)} async-done(((bf16[4,2,40,4096]{3,2,0,1:T(8,128)(2,1)}), bf16[4,2,40,4096]{3,2,0,1:T(8,128)(2,1)}, u32[]{:S(2)}, u32[]{:S(2)}) %all-to-all-start.1) | async-done | bytes 2621472 | tf_op jit(solution)/shard_map/all_to_all | solution.py:56
  90.1 3.6 copy.76
  93.7 55.5 %all-gather.2.cloned.1.call-done = bf16[3,4,4096,256]{3,2,1,0:T(8,128)(2,1)} async-done(((bf16[3,4,256,256]{3,2,1,0:T(8,128)(2,1)}), bf16[3,4,4096,256]{3,2,1,0:T(8,128)(2,1)}) %all-gather.2.cloned.1.call-update) | async-done | bytes 25165840 | tf_op jit(solution)/shard_map/all_gather | solution.py:30
  149.2 4.9 fusion.4
  154.1 5.1 fusion.2
  159.2 8.2 %fusion.8 = f32[4,4096,256]{2,1,0:T(8,128)} fusion(bf16[4,80,4096]{2,1,0:T(8,128)(2,1)S(1)} %bitcast.70, f32[4,80]{1,0:T(4,128)S(1)} %reshape.181, f32[4,80,256]{2,1,0:T(8,128)S(1)} %fusion.2, f32[4,80,256]{2,1,0:T(8,128)S(1)} %fusion.4), kind=kOutput, calls=%fused_computation.19 | convolution fusion | flops 675512320 | bytes 20055296 | tf_op jit(solution)/shard_map/esd,esf->edf/dot_general | solution.py:105
  167.7 5.8 multiply_reduce_fusion
  173.5 11.5 %fusion.36 = f32[4,4096,256]{2,1,0:T(8,128)} fusion(bf16[4,80,4096]{2,1,0:T(8,128)(2,1)S(1)} %bitcast.65, bf16[4,80,256]{2,1,0:T(8,128)(2,1)S(1)} %get-tuple-element.9), kind=kOutput, calls=%fused_computation.69 | convolution fusion | flops 671088640 | bytes 19562496 | tf_op jit(solution)/shard_map/esd,esf->edf/dot_general | solution.py:99
  185.1 10.6 %fusion.37 = f32[4,4096,256]{2,1,0:T(8,128)} fusion(bf16[4,80,4096]{2,1,0:T(8,128)(2,1)S(1)} %bitcast.66, bf16[4,80,256]{2,1,0:T(8,128)(2,1)S(1)} %get-tuple-element.10), kind=kOutput, calls=%fused_computation.70 | convolution fusion | flops 671088640 | bytes 19562496 | tf_op jit(solution)/shard_map/esd,esf->edf/dot_general | solution.py:102
  196.3 3.2 all-to-all-start.4
  199.6 6.0 fusion.1
  205.6 6.1 fusion.6
  211.7 1.7 copy.79
  213.3 3.9 all-to-all-start.3
  218.0 30.4 %all-to-all-done.3 = bf16[4,2,40,4096]{3,2,0,1:T(8,128)(2,1)S(1)} async-done(((bf16[4,2,40,4096]{3,2,0,1:T(8,128)(2,1)}), bf16[4,2,40,4096]{3,2,0,1:T(8,128)(2,1)S(1)}, u32[]{:S(2)}, u32[]{:S(2)}) %all-to-all-start.3) | async-done | bytes 2621472 | tf_op jit(solution)/shard_map/all_to_all | solution.py:92
  248.6 1.7 convolution_convert_fusion.2
  250.3 94.5 %reduce-scatter.8.cloned.1.call-done = f32[4,256,256]{2,1,0:T(8,128)} async-done(((f32[4,4096,256]{2,1,0:T(8,128)}), f32[4,256,256]{2,1,0:T(8,128)}) %reduce-scatter.8.cloned.1.call-update) | async-done | bytes 1048592 | tf_op jit(solution)/shard_map/reduce_scatter | solution.py:120
  344.8 180.6 %reduce-scatter.4.cloned.1.call-done = f32[4,256,256]{2,1,0:T(8,128)} async-done(((f32[4,4096,256]{2,1,0:T(8,128)}), f32[4,256,256]{2,1,0:T(8,128)}) %reduce-scatter.4.cloned.1.call-update) | async-done | bytes 1048592 | tf_op jit(solution)/shard_map/reduce_scatter | solution.py:118
  525.4 180.5 %reduce-scatter.6.cloned.1.call-done = f32[4,256,256]{2,1,0:T(8,128)} async-done(((f32[4,4096,256]{2,1,0:T(8,128)}), f32[4,256,256]{2,1,0:T(8,128)}) %reduce-scatter.6.cloned.1.call-update) | async-done | bytes 1048592 | tf_op jit(solution)/shard_map/reduce_scatter | solution.py:119
  705.9 8.0 %multiply_subtract_fusion = (f32[3,4,256,256]{3,2,1,0:T(8,128)}, f32[3,4,256,256]{3,2,1,0:T(8,128)}, f32[3,4,256,256]{3,2,1,0:T(8,128)}) fusion(f32[3,4,256,256]{3,2,1,0:T(8,128)} %param.11, f32[1,4,256,256]{3,2,1,0:T(8,128)} %bitcast.73, f32[1,4,256,256]{3,2,1,0:T(8,128)} %bitcast.75, f32[1,4,256,256]{3,2,1,0:T(8,128)} %bitcast.74, ...), kind=kLoop, calls=%fused_computation.17 | loop fusion | flops 13369344 | bytes 22020096 | tf_op jit(solution)/shard_map/sub | solution.py:20
  (52 shorter events, 4.6 us)
Async XLA Ops:
  7.2 10.8 %copy-start = (bf16[128,4096]{1,0:T(8,128)(2,1)S(1)}, bf16[128,4096]{1,0:T(8,128)(2,1)}, u32[]{:S(2)}) copy-start(bf16[128,4096]{1,0:T(8,128)(2,1)} %param.7) | copy-start | bytes 3145732
  7.2 3.4 copy-start.5
  7.2 3.8 copy-start.6
  7.2 142.0 %all-gather.2.cloned.1.call-start = ((), (), s32[]{:S(2)}) async-start(), calls=%async_computation.8 | async-start | bytes 26738688 | tf_op jit(solution)/shard_map/all_gather | solution.py:30
  13.2 8.0 %all-to-all-start = ((bf16[4,2,40,1]{2,0,3,1:T(4,128)(2,1)}), bf16[4,2,40,1]{2,0,3,1:T(4,128)(2,1)S(1)}, u32[]{:S(2)}, u32[]{:S(2)}) async-start(bf16[4,2,40,1]{2,0,3,1:T(4,128)(2,1)} %copy.73), calls=%async_computation | async-start | bytes 4096 | tf_op jit(solution)/shard_map/all_to_all | solution.py:59
  21.2 34.2 %all-to-all-start.2 = ((bf16[4,2,40,4096]{3,2,0,1:T(8,128)(2,1)}), bf16[4,2,40,4096]{3,2,0,1:T(8,128)(2,1)S(1)}, u32[]{:S(2)}, u32[]{:S(2)}) async-start(bf16[4,2,40,4096]{3,2,0,1:T(8,128)(2,1)} %copy.77), calls=%async_computation.2 | async-start | bytes 5242880 | tf_op jit(solution)/shard_map/all_to_all | solution.py:53
  55.4 5.2 copy-start.3
  55.4 34.7 %all-to-all-start.1 = ((bf16[4,2,40,4096]{3,2,0,1:T(8,128)(2,1)}), bf16[4,2,40,4096]{3,2,0,1:T(8,128)(2,1)}, u32[]{:S(2)}, u32[]{:S(2)}) async-start(bf16[4,2,40,4096]{3,2,0,1:T(8,128)(2,1)} %copy.75), calls=%async_computation.1 | async-start | bytes 5242880 | tf_op jit(solution)/shard_map/all_to_all | solution.py:56
  60.5 284.4 %reduce-scatter.8.cloned.1.call-start = ((), (), s32[]{:S(2)}) async-start(), calls=%async_computation.11 | async-start | bytes 17825792 | tf_op jit(solution)/shard_map/reduce_scatter | solution.py:120
  154.1 5.1 copy-start.2
  159.2 8.2 %copy-start.4 = (f32[4,80,256]{2,1,0:T(8,128)}, f32[4,80,256]{2,1,0:T(8,128)S(1)}, u32[]{:S(2)}) copy-start(f32[4,80,256]{2,1,0:T(8,128)S(1)} %fusion.2) | copy-start | bytes 983044
  167.4 358.0 %reduce-scatter.4.cloned.1.call-start = ((), (), s32[]{:S(2)}) async-start(), calls=%async_computation.9 | async-start | bytes 17825792 | tf_op jit(solution)/shard_map/reduce_scatter | solution.py:118
  185.0 520.9 %reduce-scatter.6.cloned.1.call-start = ((), (), s32[]{:S(2)}) async-start(), calls=%async_computation.10 | async-start | bytes 17825792 | tf_op jit(solution)/shard_map/reduce_scatter | solution.py:119
  196.3 17.0 %all-to-all-start.4 = ((bf16[4,2,40,1]{2,0,3,1:T(4,128)(2,1)}), bf16[4,2,40,1]{2,0,3,1:T(4,128)(2,1)S(1)}, u32[]{:S(2)}, u32[]{:S(2)}) async-start(bf16[4,2,40,1]{2,0,3,1:T(4,128)(2,1)} %copy.82), calls=%async_computation.4 | async-start | bytes 4096 | tf_op jit(solution)/shard_map/all_to_all | solution.py:95
  213.3 35.1 %all-to-all-start.3 = ((bf16[4,2,40,4096]{3,2,0,1:T(8,128)(2,1)}), bf16[4,2,40,4096]{3,2,0,1:T(8,128)(2,1)S(1)}, u32[]{:S(2)}, u32[]{:S(2)}) async-start(bf16[4,2,40,4096]{3,2,0,1:T(8,128)(2,1)} %copy.79), calls=%async_computation.3 | async-start | bytes 5242880 | tf_op jit(solution)/shard_map/all_to_all | solution.py:92
  705.9 8.0 %copy-start.1 = (bf16[128,4096]{1,0:T(8,128)(2,1)S(1)}, bf16[128,4096]{1,0:T(8,128)(2,1)}, u32[]{:S(2)}) copy-start(bf16[128,4096]{1,0:T(8,128)(2,1)} %param.7) | copy-start | bytes 3145732
Sparse Core Ops, SparseCore 0:
  10.7 138.4 all-gather.1
  167.5 177.2 reduce-scatter.7
  349.0 176.4 reduce-scatter.3
  529.4 176.4 reduce-scatter.5
where the time goes:
time: 721 us; the launch traced here: 720 us
  waiting for transfers between devices  596 us (83%)
  matrix products  63.2 us (9%)
  starting transfers between devices  20.6 us (3%)
  between operations  14 us (2%)
  local copies, waits for them, and re-layouts  13.7 us (2%)
  other arithmetic  12.7 us (2%)
    reduce_scatter x1, waiting for transfers between devices, per_device(): lax.psum_scatter(grad_gate, ('cuts', 'fsdp'), scatter_dimension=1, tiled=...  181 us
    reduce_scatter x1, waiting for transfers between devices, per_device(): lax.psum_scatter(grad_up, ('cuts', 'fsdp'), scatter_dimension=1, tiled=True)  180 us
    reduce_scatter x1, waiting for transfers between devices, per_device(): lax.psum_scatter(grad_down, ('cuts', 'fsdp'), scatter_dimension=1, tiled=...  94.5 us
    all_gather x1, waiting for transfers between devices, per_device(): lax.all_gather(params.astype(jnp.bfloat16), ('cuts', 'fsdp'), axis=2, til...  55.5 us
    all_to_all x1, waiting for transfers between devices, per_device(): lax.all_to_all(slot_grads.reshape(layout + (width,)), 'exp', split_axis=1...  30.4 us
    all_to_all x1, waiting for transfers between devices, per_device(): lax.all_to_all(send_upstream.reshape(layout + (width,)), 'exp', split_axi...  27.5 us
    all_to_all x1, waiting for transfers between devices, per_device(): lax.all_to_all(send_inputs.reshape(layout + (width,)), 'exp', split_axis=...  26.4 us
  transfers between devices with their start and end apart: 9, of which 8 were waited for; matrix products, arithmetic and copies ran while one was open for 8% of the time, Pallas kernels for 0%

commit v1 on v0

--- a/solution.py
+++ b/solution.py
@@ -27,7 +27,7 @@
     local_count = params.shape[1]
     exp_count = lax.axis_size("exp")
     capacity = 10 * token_count // 32
-    weights = lax.all_gather(params.astype(jnp.bfloat16), ("cuts", "fsdp"), axis=2, tiled=True)
+    weights = jnp.concatenate(lax.all_gather(params.astype(jnp.bfloat16), ("cuts", "fsdp")), axis=2)
     flat_ids = expert_ids.reshape(-1)
     onehot = (flat_ids[:, None] == jnp.arange(EXPERTS, dtype=jnp.int32)[None, :]).astype(jnp.int32)
     before = jnp.cumsum(onehot, axis=0) - onehot

time: 721 us -> 751 us (1.042)
  local copies, waits for them, and re-layouts: 13.7 us -> 53.9 us
    all_gather x0 -> x1, local copies, waits for them, and re-layouts: none -> 20.7 us  [per_device(): lax.all_gather(params.astype(jnp.bfloat16), ('cuts', 'fsdp'))]
    slice x1 -> x2, local copies, waits for them, and re-layouts: 0.21 us -> 12.4 us  [the longest x1 12.2 us: per_device(): w_down = weights[2]]
  transfers between devices with their start and end apart: 9 -> 9, of which waited for: 8 -> 8; matrix products, arithmetic and copies ran while one was open for 8% -> 9% of each run, Pallas kernels for 0% -> 0%
where the time goes in v1:
time: 751 us; the launch traced here: 750 us
  waiting for transfers between devices  590 us (79%)
  matrix products  56.5 us (8%)
  local copies, waits for them, and re-layouts  53.9 us (7%)
  starting transfers between devices  22.9 us (3%)
  between operations  14 us (2%)
  other arithmetic  12.7 us (2%)
    reduce_scatter x1, waiting for transfers between devices, per_device(): lax.psum_scatter(grad_gate, ('cuts', 'fsdp'), scatter_dimension=1, tiled=...  181 us
    reduce_scatter x1, waiting for transfers between devices, per_device(): lax.psum_scatter(grad_up, ('cuts', 'fsdp'), scatter_dimension=1, tiled=True)  180 us
    reduce_scatter x1, waiting for transfers between devices, per_device(): lax.psum_scatter(grad_down, ('cuts', 'fsdp'), scatter_dimension=1, tiled=...  90 us
    all_gather x1, waiting for transfers between devices, per_device(): lax.all_gather(params.astype(jnp.bfloat16), ('cuts', 'fsdp'))  53.9 us
    all_to_all x1, waiting for transfers between devices, per_device(): lax.all_to_all(slot_grads.reshape(layout + (width,)), 'exp', split_axis=1...  30.5 us
    all_to_all x1, waiting for transfers between devices, per_device(): lax.all_to_all(send_inputs.reshape(layout + (width,)), 'exp', split_axis=...  28 us
    all_to_all x1, waiting for transfers between devices, per_device(): lax.all_to_all(send_upstream.reshape(layout + (width,)), 'exp', split_axi...  26 us
    all_gather x1, local copies, waits for them, and re-layouts, per_device(): lax.all_gather(params.astype(jnp.bfloat16), ('cuts', 'fsdp'))  20.7 us
  transfers between devices with their start and end apart: 9, of which 8 were waited for; matrix products, arithmetic and copies ran while one was open for 9% of the time, Pallas kernels for 0%

profile of v1, /device:TPU:0, one launch (start us, length us, event | category | flops | bytes accessed | tf_op | source)
XLA Modules:
  0.0 750.0 jit_solution(3681823673578046628)
XLA Ops:
  7.2 3.3 convert_element_type.82
  13.2 4.3 all-to-all-start
  18.8 1.8 copy.82
  21.2 5.0 all-to-all-start.2
  27.1 1.8 copy.79
  28.9 28.0 %all-to-all-done.2 = bf16[4,2,40,4096]{3,2,0,1:T(8,128)(2,1)} async-done(((bf16[4,2,40,4096]{3,2,0,1:T(8,128)(2,1)}), bf16[4,2,40,4096]{3,2,0,1:T(8,128)(2,1)}, u32[]{:S(2)}, u32[]{:S(2)}) %all-to-all-start.2) | async-done | bytes 2621472 | tf_op jit(solution)/shard_map/all_to_all | solution.py:53
  56.8 5.1 all-to-all-start.1
  62.1 3.6 copy.83
  65.7 26.0 %all-to-all-done.1 = bf16[4,2,40,4096]{3,2,0,1:T(8,128)(2,1)} async-done(((bf16[4,2,40,4096]{3,2,0,1:T(8,128)(2,1)}), bf16[4,2,40,4096]{3,2,0,1:T(8,128)(2,1)}, u32[]{:S(2)}, u32[]{:S(2)}) %all-to-all-start.1) | async-done | bytes 2621472 | tf_op jit(solution)/shard_map/all_to_all | solution.py:56
  91.7 3.6 copy.80
  95.3 53.9 %all-gather.3.cloned.1.call-done = bf16[48,4,256,256]{3,2,1,0:T(8,128)(2,1)} async-done(((bf16[3,4,256,256]{3,2,1,0:T(8,128)(2,1)}), bf16[48,4,256,256]{3,2,1,0:T(8,128)(2,1)}) %all-gather.3.cloned.1.call-update) | async-done | bytes 25165840 | tf_op jit(solution)/shard_map/all_gather | solution.py:30
  149.2 20.7 %copy.94 = bf16[16,3,4,256,256]{4,3,0,2,1:T(8,128)(2,1)} copy(bf16[16,3,4,256,256]{4,3,2,1,0:T(8,128)(2,1)} %bitcast.70) | data formatting | bytes 50331648 | tf_op jit(solution)/shard_map/all_gather | solution.py:30
  169.8 12.2 %fusion.30 = (bf16[1,4,16,256,256]{4,3,2,1,0:T(8,128)(2,1)}, bf16[1,4,16,256,256]{4,3,2,1,0:T(8,128)(2,1)S(1)}, bf16[1,4,16,256,256]{4,3,2,1,0:T(8,128)(2,1)S(1)}) fusion(bf16[3,4,16,256,256]{4,3,2,1,0:T(8,128)(2,1)} %bitcast.60), kind=kLoop, calls=%fused_computation.62 | loop fusion | bytes 50331648 | tf_op jit(solution)/shard_map/slice | solution.py:69
  182.0 1.6 fusion.32
  183.6 1.6 copy-done.2
  185.2 1.5 fusion.31
  188.8 8.2 %fusion.2 = f32[4,4096,256]{2,1,0:T(8,128)} fusion(bf16[4,80,4096]{2,1,0:T(8,128)(2,1)S(1)} %bitcast.69, f32[4,80]{1,0:T(4,128)S(1)} %reshape.192, f32[4,80,256]{2,1,0:T(8,128)S(1)} %fusion.31, f32[4,80,256]{2,1,0:T(8,128)S(1)} %fusion.32), kind=kOutput, calls=%fused_computation.12 | convolution fusion | flops 675512320 | bytes 20055296 | tf_op jit(solution)/shard_map/esd,esf->edf/dot_general | solution.py:105
  197.2 6.0 multiply_reduce_fusion
  203.3 11.4 %fusion.34 = f32[4,4096,256]{2,1,0:T(8,128)} fusion(bf16[4,80,4096]{2,1,0:T(8,128)(2,1)S(1)} %bitcast.64, bf16[4,80,256]{2,1,0:T(8,128)(2,1)S(1)} %get-tuple-element.12), kind=kOutput, calls=%fused_computation.66 | convolution fusion | flops 671088640 | bytes 19562496 | tf_op jit(solution)/shard_map/esd,esf->edf/dot_general | solution.py:99
  214.7 11.9 %fusion.35 = f32[4,4096,256]{2,1,0:T(8,128)} fusion(bf16[4,80,4096]{2,1,0:T(8,128)(2,1)} %bitcast.61, bf16[4,80,256]{2,1,0:T(8,128)(2,1)S(1)} %get-tuple-element.13), kind=kOutput, calls=%fused_computation.67 | convolution fusion | flops 671088640 | bytes 19562496 | tf_op jit(solution)/shard_map/esd,esf->edf/dot_general | solution.py:102
  227.4 3.2 all-to-all-start.4
  230.6 6.0 fusion.33
  236.6 6.1 fusion
  242.7 1.7 copy.84
  244.3 5.0 all-to-all-start.3
  250.1 30.5 %all-to-all-done.3 = bf16[4,2,40,4096]{3,2,0,1:T(8,128)(2,1)} async-done(((bf16[4,2,40,4096]{3,2,0,1:T(8,128)(2,1)}), bf16[4,2,40,4096]{3,2,0,1:T(8,128)(2,1)}, u32[]{:S(2)}, u32[]{:S(2)}) %all-to-all-start.3) | async-done | bytes 2621472 | tf_op jit(solution)/shard_map/all_to_all | solution.py:92
  280.7 2.1 copy.85
  282.8 1.7 convolution_convert_fusion.2
  284.5 90.0 %reduce-scatter.8.cloned.1.call-done = f32[4,256,256]{2,1,0:T(8,128)} async-done(((f32[4,4096,256]{2,1,0:T(8,128)}), f32[4,256,256]{2,1,0:T(8,128)}) %reduce-scatter.8.cloned.1.call-update) | async-done | bytes 1048592 | tf_op jit(solution)/shard_map/reduce_scatter | solution.py:120
  374.4 180.6 %reduce-scatter.4.cloned.1.call-done = f32[4,256,256]{2,1,0:T(8,128)} async-done(((f32[4,4096,256]{2,1,0:T(8,128)}), f32[4,256,256]{2,1,0:T(8,128)}) %reduce-scatter.4.cloned.1.call-update) | async-done | bytes 1048592 | tf_op jit(solution)/shard_map/reduce_scatter | solution.py:118
  555.0 180.4 %reduce-scatter.6.cloned.1.call-done = f32[4,256,256]{2,1,0:T(8,128)} async-done(((f32[4,4096,256]{2,1,0:T(8,128)}), f32[4,256,256]{2,1,0:T(8,128)}) %reduce-scatter.6.cloned.1.call-update) | async-done | bytes 1048592 | tf_op jit(solution)/shard_map/reduce_scatter | solution.py:119
  735.4 8.0 %multiply_subtract_fusion = (f32[3,4,256,256]{3,2,1,0:T(8,128)}, f32[3,4,256,256]{3,2,1,0:T(8,128)}, f32[3,4,256,256]{3,2,1,0:T(8,128)}) fusion(f32[3,4,256,256]{3,2,1,0:T(8,128)} %param.11, f32[1,4,256,256]{3,2,1,0:T(8,128)} %bitcast.75, f32[1,4,256,256]{3,2,1,0:T(8,128)} %bitcast.77, f32[1,4,256,256]{3,2,1,0:T(8,128)} %bitcast.76, ...), kind=kLoop, calls=%fused_computation.10 | loop fusion | flops 13369344 | bytes 22020096 | tf_op jit(solution)/shard_map/sub | solution.py:20
  (60 shorter events, 9.4 us)
Async XLA Ops:
  7.2 10.8 %copy-start = (bf16[128,4096]{1,0:T(8,128)(2,1)S(1)}, bf16[128,4096]{1,0:T(8,128)(2,1)}, u32[]{:S(2)}) copy-start(bf16[128,4096]{1,0:T(8,128)(2,1)} %param.7) | copy-start | bytes 3145732
  7.2 3.4 copy-start.8
  7.2 3.8 copy-start.9
  7.2 142.0 %all-gather.3.cloned.1.call-start = ((), (), s32[]{:S(2)}) async-start(), calls=%async_computation.11 | async-start | bytes 26738688 | tf_op jit(solution)/shard_map/all_gather | solution.py:30
  13.2 8.0 %all-to-all-start = ((bf16[4,2,40,1]{2,0,3,1:T(4,128)(2,1)}), bf16[4,2,40,1]{2,0,3,1:T(4,128)(2,1)S(1)}, u32[]{:S(2)}, u32[]{:S(2)}) async-start(bf16[4,2,40,1]{2,0,3,1:T(4,128)(2,1)} %copy.77), calls=%async_computation | async-start | bytes 4096 | tf_op jit(solution)/shard_map/all_to_all | solution.py:59
  20.6 5.6 copy-start.7
  21.2 35.6 %all-to-all-start.2 = ((bf16[4,2,40,4096]{3,2,0,1:T(8,128)(2,1)}), bf16[4,2,40,4096]{3,2,0,1:T(8,128)(2,1)}, u32[]{:S(2)}, u32[]{:S(2)}) async-start(bf16[4,2,40,4096]{3,2,0,1:T(8,128)(2,1)} %copy.82), calls=%async_computation.2 | async-start | bytes 5242880 | tf_op jit(solution)/shard_map/all_to_all | solution.py:53
  56.8 34.9 %all-to-all-start.1 = ((bf16[4,2,40,4096]{3,2,0,1:T(8,128)(2,1)}), bf16[4,2,40,4096]{3,2,0,1:T(8,128)(2,1)}, u32[]{:S(2)}, u32[]{:S(2)}) async-start(bf16[4,2,40,4096]{3,2,0,1:T(8,128)(2,1)} %copy.79), calls=%async_computation.1 | async-start | bytes 5242880 | tf_op jit(solution)/shard_map/all_to_all | solution.py:56
  61.9 312.5 %reduce-scatter.8.cloned.1.call-start = ((), (), s32[]{:S(2)}) async-start(), calls=%async_computation.10 | async-start | bytes 17825792 | tf_op jit(solution)/shard_map/reduce_scatter | solution.py:120
  169.8 12.2 %copy-start.3 = (bf16[4,2,40,4096]{3,2,1,0:T(8,128)(2,1)S(1)}, bf16[4,2,40,4096]{3,2,1,0:T(8,128)(2,1)}, u32[]{:S(2)}) copy-start(bf16[4,2,40,4096]{3,2,1,0:T(8,128)(2,1)} %copy.83) | copy-start | bytes 7864324
  182.0 3.2 copy-start.2
  182.0 6.3 copy-start.5
  185.2 3.6 copy-start.6
  197.0 358.0 %reduce-scatter.4.cloned.1.call-start = ((), (), s32[]{:S(2)}) async-start(), calls=%async_computation.8 | async-start | bytes 17825792 | tf_op jit(solution)/shard_map/reduce_scatter | solution.py:118
  197.2 6.0 copy-start.4
  214.7 520.7 %reduce-scatter.6.cloned.1.call-start = ((), (), s32[]{:S(2)}) async-start(), calls=%async_computation.9 | async-start | bytes 17825792 | tf_op jit(solution)/shard_map/reduce_scatter | solution.py:119
  227.4 17.0 %all-to-all-start.4 = ((bf16[4,2,40,1]{2,0,3,1:T(4,128)(2,1)}), bf16[4,2,40,1]{2,0,3,1:T(4,128)(2,1)S(1)}, u32[]{:S(2)}, u32[]{:S(2)}) async-start(bf16[4,2,40,1]{2,0,3,1:T(4,128)(2,1)} %copy.87), calls=%async_computation.4 | async-start | bytes 4096 | tf_op jit(solution)/shard_map/all_to_all | solution.py:95
  244.3 36.3 %all-to-all-start.3 = ((bf16[4,2,40,4096]{3,2,0,1:T(8,128)(2,1)}), bf16[4,2,40,4096]{3,2,0,1:T(8,128)(2,1)}, u32[]{:S(2)}, u32[]{:S(2)}) async-start(bf16[4,2,40,4096]{3,2,0,1:T(8,128)(2,1)} %copy.84), calls=%async_computation.3 | async-start | bytes 5242880 | tf_op jit(solution)/shard_map/all_to_all | solution.py:92
  735.4 8.0 %copy-start.1 = (bf16[128,4096]{1,0:T(8,128)(2,1)S(1)}, bf16[128,4096]{1,0:T(8,128)(2,1)}, u32[]{:S(2)}) copy-start(bf16[128,4096]{1,0:T(8,128)(2,1)} %param.7) | copy-start | bytes 3145732
Sparse Core Ops, SparseCore 0:
  10.7 138.4 all-gather.2
  197.1 177.2 reduce-scatter.7
  378.6 176.3 reduce-scatter.3
  559.0 176.4 reduce-scatter.5
